TPU v7x, 128 devices: a whole 4x4x4 slice. The times are simulated.
128 devices in a mesh: batch: 4 (over y), expert: 8 (over x, core), tensor: 4 (over z).
Axes of the slice: x: 4, y: 4, z: 4, core: 2. Of those that a mesh axis runs over, the one named last changes fastest.
Arguments:
- tokens: bfloat16 [8, 1024, 4096], P('expert', 'batch', 'tensor'), may hold values from -8 to 8
- gain: bfloat16 [4096], P('tensor'), may hold values from 0.5 to 1.5
- phi: bfloat16 [4096, 512], P('tensor'), may hold values from -1 to 1
- w_gate: bfloat16 [8, 4096, 14336], P('expert', None, ('batch', 'tensor')), may hold values from -0.125 to 0.125
- w_up: bfloat16 [8, 4096, 14336], P('expert', None, ('batch', 'tensor')), may hold values from -0.125 to 0.125
- w_down: bfloat16 [8, 14336, 4096], P('expert', ('batch', 'tensor')), may hold values from -0.09375 to 0.09375
Outputs:
- moe_out: bfloat16 [8, 1024, 4096], P('expert', 'batch', 'tensor')
All inputs are finite; a program needn't handle non-finite values.
Results may differ from a plain program's by a relative error of at most 0.025.
Values may be sent and summed in bfloat16 or wider, within the bound.
A program may use at most 128 MiB of HBM per device.

v0:
```python
import jax
import jax.numpy as jnp
from jax import lax
from jax.sharding import PartitionSpec as P

D = 4096
P_SIZE = 64


def sent_to_all(x, axis):
    size = lax.axis_size(axis)
    return lax.all_to_all(jnp.broadcast_to(x[None], (size, *x.shape)), axis, 0, 0, tiled=True)


def of_everyone(x, axis):
    return sent_to_all(x, axis).sum(axis=0)


def packed_total(arrays, axis):
    ends = [0]
    for a in arrays:
        ends.append(ends[-1] + a.size)
    running = of_everyone(jnp.concatenate([a.ravel() for a in arrays]), axis)
    return tuple((running[b:e].reshape(a.shape) for a, b, e in zip(arrays, ends, ends[1:])))


def collected_together(x, axis):
    leaves = jax.tree.leaves(x)
    order = sorted(range(len(leaves)), key=lambda k: -leaves[k].size)
    width = (1, *leaves[order[0]].shape)[-1]
    lines = [
        jnp.pad(leaves[k].reshape(-1), (0, -leaves[k].size % width)).reshape(-1, width)
        for k in order
    ]
    both, at, found = (sent_to_all(jnp.concatenate(lines), axis), 0, {})
    for k, line in zip(order, lines):
        piece = both[:, at : at + len(line)].reshape(len(both), -1)
        found[k] = piece[:, : leaves[k].size].reshape(-1, *leaves[k].shape)
        at += len(line)
    numbers = iter(range(len(leaves)))
    return jax.tree.map(lambda _: found[next(numbers)], x)


def combined_pairwise(pieces, combine):
    while len(jax.tree.leaves(pieces)[0]) > 1:
        pieces = jax.vmap(combine)(
            *(jax.tree.map(lambda part: part[side::2], pieces) for side in (0, 1))
        )
    return jax.tree.map(lambda part: part[0], pieces)


def joined_all(x, axis, combine):
    pieces = collected_together(x, axis)
    return combined_pairwise(pieces, combine)


def cut_along(x, dim, size):
    dims = x.shape
    parts = x.reshape(*dims[:dim], size, dims[dim] // size, *dims[dim + 1 :])
    return jnp.moveaxis(parts, dim, 0)


def summed_on_arrival(x, axis, dim):
    size = lax.axis_size(axis)
    parts = lax.all_to_all(cut_along(x, dim, size), axis, 0, 0, tiled=True)
    return jnp.sum(parts.astype(jnp.float32), axis=0)


def laid_out(parts, dim):
    dims = list(parts.shape[1:])
    dims[dim] *= parts.shape[0]
    return jnp.moveaxis(parts, 0, dim).reshape(dims)


def collect(x, axis, dim):
    parts = sent_to_all(x, axis)
    return laid_out(parts, dim)


def joint_totals(left_pair, right_pair):
    new_max = jnp.maximum(left_pair[0], right_pair[0])
    merged = left_pair[1] * jnp.exp(left_pair[0] - new_max) + right_pair[1] * jnp.exp(
        right_pair[0] - new_max
    )
    return (new_max, merged)


def local(tokens, gain, phi, w_gate, w_up, w_down):
    tokens_f = tokens[0].astype(jnp.float32)
    gain_f = gain.astype(jnp.float32)
    scaled = (tokens_f * gain_f[None, :]).astype(jnp.bfloat16)
    squares = jnp.sum(tokens_f * tokens_f, axis=1)
    partial_logits = jnp.dot(scaled, phi, preferred_element_type=jnp.float32)
    squares, partial_logits = packed_total((squares, partial_logits), "tensor")
    inv_rms = lax.rsqrt(squares / D + 1e-06)
    logits = partial_logits * inv_rms[:, None]
    normed = (tokens_f * gain_f[None, :] * inv_rms[:, None]).astype(jnp.bfloat16)
    combine = jax.nn.softmax(logits, axis=1).astype(jnp.bfloat16)
    local_max = jnp.max(logits, axis=0)
    local_total = jnp.sum(jnp.exp(logits - local_max[None, :]), axis=0)
    column_max, column_total = joined_all((local_max, local_total), "batch", joint_totals)
    dispatch = (jnp.exp(logits - column_max[None, :]) / column_total[None, :]).astype(jnp.bfloat16)
    slot_partial = jnp.einsum("ts,td->sd", dispatch, normed, preferred_element_type=jnp.float32)
    per_device = w_gate.shape[0]
    experts = phi.shape[1] // P_SIZE
    width_share = tokens.shape[2]
    slot_partial = slot_partial.reshape(experts, P_SIZE, width_share)
    quarter = summed_on_arrival(slot_partial.astype(jnp.bfloat16), "batch", 1).astype(jnp.bfloat16)
    exchanged = lax.all_to_all(quarter, "expert", split_axis=0, concat_axis=0, tiled=True)
    arrived = collect(exchanged, "batch", 1)
    groups = arrived.shape[0] // per_device
    arrived = arrived.reshape(groups, per_device, P_SIZE, width_share)
    hidden_share = w_gate.shape[2]
    shard_piece = lax.all_gather(arrived, "tensor", axis=3, tiled=True)
    gate_next = jnp.einsum(
        "gxpd,xdf->gxpf", shard_piece, w_gate, preferred_element_type=jnp.float32
    )
    up_next = jnp.einsum("gxpd,xdf->gxpf", shard_piece, w_up, preferred_element_type=jnp.float32)
    hidden = (jax.nn.silu(gate_next) * up_next).astype(jnp.bfloat16)
    batch_count = lax.axis_size("batch")
    tensor_count = lax.axis_size("tensor")
    hidden = hidden.reshape(groups, per_device, batch_count, P_SIZE // batch_count, hidden_share)
    down_split = w_down.reshape(per_device, hidden_share, tensor_count, D // tensor_count)
    partials = jnp.einsum(
        "gxbqf,xftd->btgxqd", hidden, down_split, preferred_element_type=jnp.float32
    )
    partials = partials.reshape(
        batch_count * tensor_count, groups, per_device, P_SIZE // batch_count, width_share
    ).astype(jnp.bfloat16)
    summed = summed_on_arrival(partials, ("batch", "tensor"), 0)
    slot_out = summed[0].astype(jnp.bfloat16)
    returned = lax.all_to_all(slot_out, "expert", split_axis=0, concat_axis=0, tiled=True)
    returned = returned.reshape(experts, P_SIZE // batch_count, width_share)
    returned = collect(returned, "batch", 1)
    moe_out = jnp.dot(
        combine, returned.reshape(experts * P_SIZE, width_share), preferred_element_type=jnp.float32
    )
    return moe_out.astype(jnp.bfloat16)[None]


def solution(mesh):
    placed = (
        P("expert", "batch", "tensor"),
        P("tensor"),
        P("tensor", None),
        P("expert", None, ("batch", "tensor")),
        P("expert", None, ("batch", "tensor")),
        P("expert", ("batch", "tensor"), None),
    )
    return jax.shard_map(
        local, mesh=mesh, in_specs=placed, out_specs=P("expert", "batch", "tensor"), check_vma=False
    )
```

profile of v0, /device:TPU:0, one launch (start us, length us, event | category | flops | bytes accessed | tf_op | source)
XLA Modules:
  0.0 282.4 jit_solution(13784396119925911884)
XLA Ops:
  6.5 1.3 fusion.22
  7.9 0.7 convert_element_type.86
  8.5 1.5 convolution_bitcast_fusion
  10.0 0.1 copy.46
  10.2 2.5 broadcast_in_dim.12
  12.8 31.6 %all_to_all.41 = f32[4,1,131328]{2,1,0:T(1,128)S(1)} all-to-all(f32[4,1,131328]{2,1,0:T(1,128)S(1)} %broadcast_in_dim.12), channel_id=1, replica_groups=mesh['batch'=4,'expert'=8,'tensor'=4] {'tensor'}, dimensions={0} | all-to-all | bytes 4202496 | tf_op jit(solution)/shard_map/all_to_all | solution.py:12
  44.4 10.6 %reduce_sum.61 = f32[131328]{0:T(1024)} reduce(f32[4,1,131328]{2,1,0:T(1,128)S(1)} %all_to_all.41, f32[]{:T(128)} %constant.6.clone.1), dimensions={0,1}, to_apply=%region_1.0 | reduce | flops 393984 | bytes 2626564 | tf_op jit(solution)/shard_map/reduce_sum | solution.py:16
  55.0 0.7 fusion.35
  55.7 1.1 slice.52
  56.7 0.1 reshape.121
  56.8 0.2 multiply_reduce_fusion
  57.0 0.3 exponential_reduce_fusion
  57.4 9.6 %all_to_all.42 = f32[4,2,512]{2,1,0:T(2,128)S(1)} all-to-all(f32[4,2,512]{2,1,0:T(2,128)S(1)} %broadcast_in_dim.13), channel_id=1, replica_groups=mesh['batch'=4,'expert'=8,'tensor'=4] {'batch'}, dimensions={0} | all-to-all | bytes 32768 | tf_op jit(solution)/shard_map/all_to_all | solution.py:12
  67.2 0.2 fusion.32
  67.4 0.1 copy.31
  67.5 0.0 copy-done.2
  67.5 0.5 convolution_convert_fusion
  68.0 0.1 copy.57
  68.1 15.2 %all_to_all.43 = bf16[4,8,16,1024]{3,2,1,0:T(8,128)(2,1)S(1)} all-to-all(bf16[4,8,16,1024]{3,2,1,0:T(8,128)(2,1)S(1)} %bitcast.118), channel_id=1, replica_groups=mesh['batch'=4,'expert'=8,'tensor'=4] {'batch'}, dimensions={0} | all-to-all | bytes 2097152 | tf_op jit(solution)/shard_map/all_to_all | solution.py:65
  83.3 0.2 reduce_sum.64
  83.5 11.6 %all_to_all.44 = bf16[8,16,1024]{2,1,0:T(8,128)(2,1)S(1)} all-to-all(bf16[8,16,1024]{2,1,0:T(8,128)(2,1)S(1)} %reduce_sum.64), channel_id=1, replica_groups=mesh['batch'=4,'expert'=8,'tensor'=4] {'expert'}, dimensions={0} | all-to-all | bytes 524288 | tf_op jit(solution)/shard_map/all_to_all | solution.py:109
  95.1 0.1 broadcast_in_dim.14
  95.2 17.4 %all_to_all.45 = bf16[4,8,16,1024]{3,2,1,0:T(8,128)(2,1)S(1)} all-to-all(bf16[4,8,16,1024]{3,2,1,0:T(8,128)(2,1)S(1)} %broadcast_in_dim.14), channel_id=1, replica_groups=mesh['batch'=4,'expert'=8,'tensor'=4] {'batch'}, dimensions={0} | all-to-all | bytes 2097152 | tf_op jit(solution)/shard_map/all_to_all | solution.py:12
  112.6 1.0 copy.33
  113.7 0.0 all-gather.2.cloned.1.call-update
  113.7 13.1 %reshape.131 = bf16[896,4,1024]{2,1,0:T(4,128)(2,1)} reshape(bf16[1,896,4096]{2,1,0:T(8,128)(2,1)} %param.11) | data formatting | bytes 14680064 | tf_op jit(solution)/shard_map/reshape.6
  126.8 31.1 %all-gather.2.cloned.1.call-done = bf16[8,1,64,4096]{3,2,0,1:T(8,128)(2,1)} async-done(((bf16[8,1,64,1024]{3,2,0,1:T(8,128)(2,1)}), bf16[8,1,64,4096]{3,2,0,1:T(8,128)(2,1)}) %all-gather.2.cloned.1.call-update) | async-done | bytes 4194320 | tf_op jit(solution)/shard_map/all_gather | solution.py:114
  157.9 10.5 %fusion.4 = f32[8,64,896]{2,1,0:T(8,128)S(1)} fusion(bf16[1,4096,896]{2,1,0:T(8,128)(2,1)} %param.9, bf16[8,1,64,4096]{3,2,0,1:T(8,128)(2,1)} %all-gather.2.cloned.1.call-done), kind=kOutput, calls=%fused_computation.4 | convolution fusion | flops 3758096384 | bytes 13369344 | tf_op jit(solution)/shard_map/gxpd,xdf->gxpf/dot_general | solution.py:115
  168.5 0.0 slice-start.1
  168.5 7.8 %fusion.11 = bf16[8,1,64,896]{3,2,0,1:T(8,128)(2,1)S(1)} fusion(f32[8,64,896]{2,1,0:T(8,128)S(1)} %fusion.4, bf16[1,4096,896]{2,1,0:T(8,128)(2,1)} %param.10, bf16[8,1,64,4096]{3,2,0,1:T(8,128)(2,1)S(1)} %copy-done.4), kind=kOutput, calls=%fused_computation.10 | convolution fusion | flops 3760848896 | bytes 14286848 | tf_op jit(solution)/shard_map/gxpd,xdf->gxpf/dot_general | solution.py:118
  176.2 0.0 slice-done
  176.3 5.6 %fusion.8 = bf16[8,4,16,4,1024]{4,2,3,1,0:T(8,128)(2,1)S(1)} fusion(bf16[8,4,16,896,1]{3,2,4,1,0:T(8,128)(2,1)S(1)} %bitcast.130, bf16[896,4,1024,1,1]{2,1,0,4,3:T(4,128)(2,1)S(1)} %bitcast.113), kind=kOutput, calls=%fused_computation.8 | convolution fusion | flops 3760193536 | bytes 12451840 | tf_op jit(solution)/shard_map/gxbqf,xftd->btgxqd/dot_general | solution.py:124
  181.9 0.4 copy.35
  182.4 56.5 %all_to_all.46 = bf16[16,1,8,1,16,1024]{5,4,2,3,1,0:T(8,128)(2,1)} all-to-all(bf16[16,1,8,1,16,1024]{5,4,2,3,1,0:T(8,128)(2,1)S(1)} %copy.35), channel_id=1, replica_groups=mesh['batch'=4,'expert'=8,'tensor'=4] {'batch','tensor'}, dimensions={0} | all-to-all | bytes 8388608 | tf_op jit(solution)/shard_map/all_to_all | solution.py:65
  238.8 3.9 %reduce_sum.65 = bf16[8,16,1024]{2,1,0:T(8,128)(2,1)} reduce(bf16[16,1,8,1,16,1024]{5,4,2,3,1,0:T(8,128)(2,1)} %all_to_all.46, bf16[]{:T(256)} %constant.15.clone.1), dimensions={0,1,3}, to_apply=%region_7.8 | reduce | flops 1966080 | bytes 4456450 | tf_op jit(solution)/shard_map/reduce_sum | solution.py:66
  242.7 4.4 %all-to-all-start.6 = ((bf16[8,1,16,1024]{3,2,1,0:T(8,128)(2,1)}), bf16[8,1,16,1024]{3,2,1,0:T(8,128)(2,1)S(1)}, u32[]{:S(2)}, u32[]{:S(2)}) async-start(bf16[8,1,16,1024]{3,2,1,0:T(8,128)(2,1)} %bitcast.35), calls=%async_computation.6 | async-start | bytes 524288 | tf_op jit(solution)/shard_map/all_to_all | solution.py:132
  247.1 0.1 broadcast_bitcast_fusion
  247.2 0.9 copy.49
  248.1 1.0 copy.48
  249.1 0.9 copy.47
  250.0 4.6 %all-to-all-done.6 = bf16[8,1,16,1024]{3,2,1,0:T(8,128)(2,1)S(1)} async-done(((bf16[8,1,16,1024]{3,2,1,0:T(8,128)(2,1)}), bf16[8,1,16,1024]{3,2,1,0:T(8,128)(2,1)S(1)}, u32[]{:S(2)}, u32[]{:S(2)}) %all-to-all-start.6) | async-done | bytes 262176 | tf_op jit(solution)/shard_map/all_to_all | solution.py:132
  254.6 1.1 broadcast_in_dim.16
  255.7 3.5 %all-to-all-start.7 = ((bf16[4,8,16,1024]{3,2,1,0:T(8,128)(2,1)}), bf16[4,8,16,1024]{3,2,1,0:T(8,128)(2,1)S(1)}, u32[]{:S(2)}, u32[]{:S(2)}) async-start(bf16[4,8,16,1024]{3,2,1,0:T(8,128)(2,1)} %broadcast_in_dim.16), calls=%async_computation.7 | async-start | bytes 2097152 | tf_op jit(solution)/shard_map/all_to_all | solution.py:12
  259.3 1.5 divide_convert_fusion.1
  260.8 0.2 convert_element_type.89
  260.9 13.3 %all-to-all-done.7 = bf16[4,8,16,1024]{3,2,1,0:T(8,128)(2,1)S(1)} async-done(((bf16[4,8,16,1024]{3,2,1,0:T(8,128)(2,1)}), bf16[4,8,16,1024]{3,2,1,0:T(8,128)(2,1)S(1)}, u32[]{:S(2)}, u32[]{:S(2)}) %all-to-all-start.7) | async-done | bytes 1048608 | tf_op jit(solution)/shard_map/all_to_all | solution.py:12
  274.2 0.1 copy.36
  274.3 1.2 fusion.21
  (24 shorter events, 0.2 us)
Async XLA Ops:
  6.5 2.0 copy-start
  6.5 151.4 %all-gather.2.cloned.1.call-start = ((), (), s32[]{:S(2)}) async-start(), calls=%async_computation.8 | async-start | bytes 5242880 | tf_op jit(solution)/shard_map/all_gather | solution.py:114
  44.4 23.1 %copy-start.2 = (bf16[1,256,1024]{2,1,0:T(8,128)(2,1)S(1)}, bf16[1,256,1024]{2,1,0:T(8,128)(2,1)}, u32[]{:S(2)}) copy-start(bf16[1,256,1024]{2,1,0:T(8,128)(2,1)} %param.6) | copy-start | bytes 1572868
  157.9 10.5 %copy-start.4 = (bf16[8,1,64,4096]{3,2,0,1:T(8,128)(2,1)S(1)}, bf16[8,1,64,4096]{3,2,0,1:T(8,128)(2,1)}, u32[]{:S(2)}) copy-start(bf16[8,1,64,4096]{3,2,0,1:T(8,128)(2,1)} %all-gather.2.cloned.1.call-done) | copy-start | bytes 12582916
  157.9 18.3 %slice-start = ((s8[7340032]{0:T(1024)(128)(4,1)}), s8[4194304]{0:T(1024)(128)(4,1)S(1)}, s32[]{:S(2)}) async-start(s8[7340032]{0:T(1024)(128)(4,1)} %bitcast.111), calls=%async_computation.9 | async-start | bytes 8388608
  168.5 7.8 %slice-start.1 = ((s8[7340032]{0:T(1024)(128)(4,1)}), s8[3145728]{0:T(1024)(128)(4,1)S(1)}, s32[]{:S(2)}) async-start(s8[7340032]{0:T(1024)(128)(4,1)} %bitcast.111), calls=%async_computation.10 | async-start | bytes 6291456
  242.7 16.5 %copy-start.3 = (f32[131328]{0:T(1024)S(1)}, f32[131328]{0:T(1024)}, u32[]{:S(2)}) copy-start(f32[131328]{0:T(1024)} %reduce_sum.61) | copy-start | bytes 1575940
  242.7 11.9 %all-to-all-start.6 = ((bf16[8,1,16,1024]{3,2,1,0:T(8,128)(2,1)}), bf16[8,1,16,1024]{3,2,1,0:T(8,128)(2,1)S(1)}, u32[]{:S(2)}, u32[]{:S(2)}) async-start(bf16[8,1,16,1024]{3,2,1,0:T(8,128)(2,1)} %bitcast.35), calls=%async_computation.6 | async-start | bytes 524288 | tf_op jit(solution)/shard_map/all_to_all | solution.py:132
  254.6 21.0 %copy-start.1 = (bf16[1024,512]{1,0:T(8,128)(2,1)S(1)}, bf16[1024,512]{1,0:T(8,128)(2,1)}, u32[]{:S(2)}) copy-start(bf16[1024,512]{1,0:T(8,128)(2,1)} %param.8) | copy-start | bytes 3145732
  255.7 18.5 %all-to-all-start.7 = ((bf16[4,8,16,1024]{3,2,1,0:T(8,128)(2,1)}), bf16[4,8,16,1024]{3,2,1,0:T(8,128)(2,1)S(1)}, u32[]{:S(2)}, u32[]{:S(2)}) async-start(bf16[4,8,16,1024]{3,2,1,0:T(8,128)(2,1)} %broadcast_in_dim.16), calls=%async_computation.7 | async-start | bytes 2097152 | tf_op jit(solution)/shard_map/all_to_all | solution.py:12
Sparse Core Ops, SparseCore 0:
  113.8 44.0 all-gather.1
where the time goes:
time: 283 us; the launch traced here: 282 us
  blocking collectives  142 us (50%)
  waiting for transfers between devices  49 us (17%)
  matrix products  27.2 us (10%)
  local copies, waits for them, and re-layouts  23.2 us (8%)
  other arithmetic  19.6 us (7%)
  between operations  13.7 us (5%)
  starting transfers between devices  7.9 us (3%)
    all_to_all x2, blocking collectives, summed_on_arrival(): parts = lax.all_to_all(cut_along(x, dim, size), axis, 0, 0, tiled=True)  71.6 us
    all_to_all x3, blocking collectives, sent_to_all(): lax.all_to_all(jnp.broadcast_to(x[None], (size, *x.shape)), axis, 0, 0, t...  58.7 us
    all_gather x1, waiting for transfers between devices, local(): shard_piece = lax.all_gather(arrived, 'tensor', axis=3, tiled=True)  31.1 us
    all_to_all x1, waiting for transfers between devices, sent_to_all(): lax.all_to_all(jnp.broadcast_to(x[None], (size, *x.shape)), axis, 0, 0, t...  13.3 us
    another operation x1, local copies, waits for them, and re-layouts  13.1 us
    all_to_all x1, blocking collectives, local(): lax.all_to_all(quarter, 'expert', split_axis=0, concat_axis=0, tiled=True)  11.6 us
    reduce_sum x1, other arithmetic, of_everyone(): return sent_to_all(x, axis).sum(axis=0)  10.6 us
    dot_general x1, matrix products, local(): jnp.einsum('gxpd,xdf->gxpf', shard_piece, w_gate, preferred_element_type=...  10.5 us
  transfers between devices with their start and end apart: 3, of which 3 were waited for; matrix products, arithmetic and copies ran while one was open for 6% of the time, Pallas kernels for 0%

commit v1 on v0

--- a/solution.py
+++ b/solution.py
@@ -5,6 +5,29 @@
 
 D = 4096
 P_SIZE = 64
+
+
+def track_tracks(inp):
+    front, outer, known = (lax.axis_size("tensor"), lax.axis_index("tensor"), inp.shape[3])
+    trail = [(q, (q + 1) % front) for q in range(front)]
+    piece_next = jnp.zeros((*inp.shape[:3], front * known, *inp.shape[4:]), inp.dtype)
+    frames = [(q, (q - 1) % front) for q in range(front)]
+    piece_next = lax.dynamic_update_slice_in_dim(piece_next, inp, outer * known, axis=3)
+    high = r1 = inp
+    j = 1
+    current_block = front // 2
+    while j < current_block + 1:
+        high = lax.ppermute(high, "tensor", trail)
+        piece_next = lax.dynamic_update_slice_in_dim(
+            piece_next, high, (outer - j) % front * known, axis=3
+        )
+        if j < front - current_block:
+            r1 = lax.ppermute(r1, "tensor", frames)
+            piece_next = lax.dynamic_update_slice_in_dim(
+                piece_next, r1, (outer + j) % front * known, axis=3
+            )
+        j = j + 1
+    return piece_next
 
 
 def sent_to_all(x, axis):
@@ -111,7 +134,7 @@
     groups = arrived.shape[0] // per_device
     arrived = arrived.reshape(groups, per_device, P_SIZE, width_share)
     hidden_share = w_gate.shape[2]
-    shard_piece = lax.all_gather(arrived, "tensor", axis=3, tiled=True)
+    shard_piece = track_tracks(arrived)
     gate_next = jnp.einsum(
         "gxpd,xdf->gxpf", shard_piece, w_gate, preferred_element_type=jnp.float32
     )

time: 283 us -> 265 us (0.936)
  between operations: 13.7 us -> 0.35 us
  matrix products: 27.2 us -> 22.1 us
  blocking collectives: 142 us -> 137 us
    all_gather x1 -> x0, waiting for transfers between devices: 31.1 us -> none  [local(): shard_piece = lax.all_gather(arrived, 'tensor', axis=3, tiled=True)]
    ppermute x0 -> x3, waiting for transfers between devices: none -> 30.9 us  [the longest x2 30.9 us: track_tracks(): high = lax.ppermute(high, 'tensor', trail)]
    all_to_all x2, blocking collectives: 71.6 us -> 66.5 us  [summed_on_arrival(): parts = lax.all_to_all(cut_along(x, dim, size), axis, 0, 0, tiled=True)]
    ppermute x0 -> x3, starting transfers between devices: none -> 3.31 us  [the longest x1 2.67 us: track_tracks(): r1 = lax.ppermute(r1, 'tensor', frames)]
    dot_general x1, matrix products: 7.75 us -> 4.59 us  [local(): jnp.einsum('gxpd,xdf->gxpf', shard_piece, w_up, preferred_element_type=jn...]
    dynamic_update_slice x0 -> x4, local copies, waits for them, and re-layouts: none -> 3.04 us  [the longest x2 1.59 us: track_tracks(): lax.dynamic_update_slice_in_dim(piece_next, high, (outer - j) % front * k...]
    another operation x1 -> x2, local copies, waits for them, and re-layouts: 13.1 us -> 13.3 us
  transfers between devices with their start and end apart: 3 -> 5, of which waited for: 3 -> 4; matrix products, arithmetic and copies ran while one was open for 6% -> 7% of each run, Pallas kernels for 0% -> 0%
where the time goes in v1:
time: 265 us; the launch traced here: 264 us
  blocking collectives  137 us (52%)
  waiting for transfers between devices  48.7 us (18%)
  local copies, waits for them, and re-layouts  25.5 us (10%)
  matrix products  22.1 us (8%)
  other arithmetic  19.6 us (7%)
  starting transfers between devices  10.6 us (4%)
    all_to_all x2, blocking collectives, summed_on_arrival(): parts = lax.all_to_all(cut_along(x, dim, size), axis, 0, 0, tiled=True)  66.5 us
    all_to_all x3, blocking collectives, sent_to_all(): lax.all_to_all(jnp.broadcast_to(x[None], (size, *x.shape)), axis, 0, 0, t...  58.7 us
    ppermute x2, waiting for transfers between devices, track_tracks(): high = lax.ppermute(high, 'tensor', trail)  30.9 us
    another operation x2, local copies, waits for them, and re-layouts  13.3 us
    all_to_all x1, waiting for transfers between devices, sent_to_all(): lax.all_to_all(jnp.broadcast_to(x[None], (size, *x.shape)), axis, 0, 0, t...  13.3 us
    all_to_all x1, blocking collectives, local(): lax.all_to_all(quarter, 'expert', split_axis=0, concat_axis=0, tiled=True)  11.6 us
    reduce_sum x1, other arithmetic, of_everyone(): return sent_to_all(x, axis).sum(axis=0)  10.5 us
    dot_general x1, matrix products, local(): jnp.einsum('gxpd,xdf->gxpf', shard_piece, w_gate, preferred_element_type=...  8.68 us
  transfers between devices with their start and end apart: 5, of which 4 were waited for; matrix products, arithmetic and copies ran while one was open for 7% of the time, Pallas kernels for 0%

profile of v1, /device:TPU:0, one launch (start us, length us, event | category | flops | bytes accessed | tf_op | source)
XLA Modules:
  0.0 263.7 jit_solution(7778050350489611703)
XLA Ops:
  0.0 0.8 convert_element_type.86
  0.8 1.2 fusion.18
  2.0 1.5 convolution_bitcast_fusion
  3.5 0.1 copy.52
  3.7 2.5 broadcast_in_dim.12
  6.2 31.6 %all_to_all.41 = f32[4,1,131328]{2,1,0:T(1,128)S(1)} all-to-all(f32[4,1,131328]{2,1,0:T(1,128)S(1)} %broadcast_in_dim.12), channel_id=1, replica_groups=mesh['batch'=4,'expert'=8,'tensor'=4] {'tensor'}, dimensions={0} | all-to-all | bytes 4202496 | tf_op jit(solution)/shard_map/all_to_all | solution.py:35
  37.9 10.5 %reduce_sum.61 = f32[131328]{0:T(1024)} reduce(f32[4,1,131328]{2,1,0:T(1,128)S(1)} %all_to_all.41, f32[]{:T(128)} %constant.43.clone.1), dimensions={0,1}, to_apply=%region_1.0 | reduce | flops 393984 | bytes 2626564 | tf_op jit(solution)/shard_map/reduce_sum | solution.py:39
  48.4 1.1 slice.52
  49.5 0.7 fusion.31
  50.2 0.2 multiply_reduce_fusion
  50.4 0.3 exponential_reduce_fusion
  50.8 9.6 %all_to_all.42 = f32[4,2,512]{2,1,0:T(2,128)S(1)} all-to-all(f32[4,2,512]{2,1,0:T(2,128)S(1)} %broadcast_in_dim.13), channel_id=1, replica_groups=mesh['batch'=4,'expert'=8,'tensor'=4] {'batch'}, dimensions={0} | all-to-all | bytes 32768 | tf_op jit(solution)/shard_map/all_to_all | solution.py:35
  60.6 0.2 fusion.28
  60.8 0.1 copy.37
  60.9 0.5 convolution_convert_fusion
  61.5 15.2 %all_to_all.43 = bf16[4,8,16,1024]{3,2,1,0:T(8,128)(2,1)S(1)} all-to-all(bf16[4,8,16,1024]{3,2,1,0:T(8,128)(2,1)S(1)} %bitcast.124), channel_id=1, replica_groups=mesh['batch'=4,'expert'=8,'tensor'=4] {'batch'}, dimensions={0} | all-to-all | bytes 2097152 | tf_op jit(solution)/shard_map/all_to_all | solution.py:88
  76.7 0.2 reduce_sum.64
  76.9 11.6 %all_to_all.44 = bf16[8,16,1024]{2,1,0:T(8,128)(2,1)S(1)} all-to-all(bf16[8,16,1024]{2,1,0:T(8,128)(2,1)S(1)} %reduce_sum.64), channel_id=1, replica_groups=mesh['batch'=4,'expert'=8,'tensor'=4] {'expert'}, dimensions={0} | all-to-all | bytes 524288 | tf_op jit(solution)/shard_map/all_to_all | solution.py:132
  88.5 0.1 broadcast_in_dim.14
  88.6 17.4 %all_to_all.45 = bf16[4,8,16,1024]{3,2,1,0:T(8,128)(2,1)S(1)} all-to-all(bf16[4,8,16,1024]{3,2,1,0:T(8,128)(2,1)S(1)} %broadcast_in_dim.14), channel_id=1, replica_groups=mesh['batch'=4,'expert'=8,'tensor'=4] {'batch'}, dimensions={0} | all-to-all | bytes 2097152 | tf_op jit(solution)/shard_map/all_to_all | solution.py:35
  106.1 0.6 collective-permute-start
  106.8 2.7 %collective-permute-start.1 = (bf16[8,1,64,1024]{3,2,0,1:T(8,128)(2,1)S(1)}, bf16[8,1,64,1024]{3,2,0,1:T(8,128)(2,1)}, u32[]{:S(2)}, u32[]{:S(2)}) collective-permute-start(bf16[8,1,64,1024]{3,2,0,1:T(8,128)(2,1)S(1)} %bitcast.119), channel_id=1, source_target_pairs={{0,3},{1,0},{2,1},{3,2},{4,7},{5,4},{6,5},{7,6},{8,11},{9,8},{10,9... | collective-permute-start | bytes 3145736 | tf_op jit(solution)/shard_map/ppermute | solution.py:25
  109.4 21.6 %collective-permute-done = bf16[8,1,64,1024]{3,2,0,1:T(8,128)(2,1)S(1)} collective-permute-done((bf16[8,1,64,1024]{3,2,0,1:T(8,128)(2,1)S(1)}, bf16[8,1,64,1024]{3,2,0,1:T(8,128)(2,1)S(1)}, u32[]{:S(2)}, u32[]{:S(2)}) %collective-permute-start) | collective-permute-done | bytes 1048608 | tf_op jit(solution)/shard_map/ppermute | solution.py:20
  131.1 12.8 %reshape.149 = bf16[896,4,1024]{2,1,0:T(4,128)(2,1)} reshape(bf16[1,896,4096]{2,1,0:T(8,128)(2,1)} %param.11) | data formatting | bytes 14680064 | tf_op jit(solution)/shard_map/reshape.6
  143.9 0.5 broadcast.40
  144.4 0.1 constant_dynamic-update-slice_fusion
  144.6 0.1 bitcast_dynamic-update-slice_fusion.2
  144.7 1.3 bitcast_dynamic-update-slice_fusion.1
  146.0 9.2 %collective-permute-done.2 = bf16[8,1,64,1024]{3,2,0,1:T(8,128)(2,1)} collective-permute-done((bf16[8,1,64,1024]{3,2,0,1:T(8,128)(2,1)S(1)}, bf16[8,1,64,1024]{3,2,0,1:T(8,128)(2,1)}, u32[]{:S(2)}, u32[]{:S(2)}) %collective-permute-start.2) | collective-permute-done | bytes 1048608 | tf_op jit(solution)/shard_map/ppermute | solution.py:20
  155.2 1.5 bitcast_dynamic-update-slice_fusion
  156.7 8.7 %fusion.4 = f32[8,64,896]{2,1,0:T(8,128)S(1)} fusion(bf16[8,64,4096]{2,1,0:T(8,128)(2,1)S(1)} %bitcast_dynamic-update-slice_fusion, bf16[1,4096,896]{2,1,0:T(8,128)(2,1)} %param.9), kind=kOutput, calls=%fused_computation.4 | convolution fusion | flops 3758096384 | bytes 13369344 | tf_op jit(solution)/shard_map/gxpd,xdf->gxpf/dot_general | solution.py:138
  165.5 4.6 %fusion.9 = bf16[8,1,64,896]{3,2,0,1:T(8,128)(2,1)S(1)} fusion(f32[8,64,896]{2,1,0:T(8,128)S(1)} %fusion.4, bf16[8,64,4096]{2,1,0:T(8,128)(2,1)S(1)} %bitcast_dynamic-update-slice_fusion, bf16[1,4096,896]{2,1,0:T(8,128)(2,1)S(1)} %bitcast.136), kind=kOutput, calls=%fused_computation.8 | convolution fusion | flops 3760848896 | bytes 14286848 | tf_op jit(solution)/shard_map/gxpd,xdf->gxpf/dot_general | solution.py:141
  170.1 5.6 %fusion.6 = bf16[8,4,16,4,1024]{4,2,3,1,0:T(8,128)(2,1)S(1)} fusion(bf16[8,4,16,896,1]{3,2,4,1,0:T(8,128)(2,1)S(1)} %bitcast.137, bf16[896,4,1024,1,1]{2,1,0,4,3:T(4,128)(2,1)S(1)} %bitcast.117), kind=kOutput, calls=%fused_computation.6 | convolution fusion | flops 3760193536 | bytes 12451840 | tf_op jit(solution)/shard_map/gxbqf,xftd->btgxqd/dot_general | solution.py:147
  175.7 0.4 copy.41
  176.2 51.4 %all_to_all.46 = bf16[16,1,8,1,16,1024]{5,4,2,3,1,0:T(8,128)(2,1)} all-to-all(bf16[16,1,8,1,16,1024]{5,4,2,3,1,0:T(8,128)(2,1)S(1)} %copy.41), channel_id=1, replica_groups=mesh['batch'=4,'expert'=8,'tensor'=4] {'batch','tensor'}, dimensions={0} | all-to-all | bytes 8388608 | tf_op jit(solution)/shard_map/all_to_all | solution.py:88
  227.6 3.9 %reduce_sum.65 = bf16[8,16,1024]{2,1,0:T(8,128)(2,1)} reduce(bf16[16,1,8,1,16,1024]{5,4,2,3,1,0:T(8,128)(2,1)} %all_to_all.46, bf16[]{:T(256)} %constant.47.clone.1), dimensions={0,1,3}, to_apply=%region_7.8 | reduce | flops 1966080 | bytes 4456450 | tf_op jit(solution)/shard_map/reduce_sum | solution.py:89
  231.4 3.8 %all-to-all-start.6 = ((bf16[8,1,16,1024]{3,2,1,0:T(8,128)(2,1)}), bf16[8,1,16,1024]{3,2,1,0:T(8,128)(2,1)S(1)}, u32[]{:S(2)}, u32[]{:S(2)}) async-start(bf16[8,1,16,1024]{3,2,1,0:T(8,128)(2,1)} %bitcast.39), calls=%async_computation.6 | async-start | bytes 524288 | tf_op jit(solution)/shard_map/all_to_all | solution.py:155
  235.4 0.9 copy.55
  236.3 0.9 copy.54
  237.2 0.9 copy.53
  238.1 4.6 %all-to-all-done.6 = bf16[8,1,16,1024]{3,2,1,0:T(8,128)(2,1)S(1)} async-done(((bf16[8,1,16,1024]{3,2,1,0:T(8,128)(2,1)}), bf16[8,1,16,1024]{3,2,1,0:T(8,128)(2,1)S(1)}, u32[]{:S(2)}, u32[]{:S(2)}) %all-to-all-start.6) | async-done | bytes 262176 | tf_op jit(solution)/shard_map/all_to_all | solution.py:155
  242.8 1.1 broadcast_in_dim.16
  243.9 3.5 %all-to-all-start.7 = ((bf16[4,8,16,1024]{3,2,1,0:T(8,128)(2,1)}), bf16[4,8,16,1024]{3,2,1,0:T(8,128)(2,1)S(1)}, u32[]{:S(2)}, u32[]{:S(2)}) async-start(bf16[4,8,16,1024]{3,2,1,0:T(8,128)(2,1)} %broadcast_in_dim.16), calls=%async_computation.7 | async-start | bytes 2097152 | tf_op jit(solution)/shard_map/all_to_all | solution.py:35
  247.4 1.5 divide_convert_fusion.1
  248.9 0.2 convert_element_type.89
  249.1 13.3 %all-to-all-done.7 = bf16[4,8,16,1024]{3,2,1,0:T(8,128)(2,1)S(1)} async-done(((bf16[4,8,16,1024]{3,2,1,0:T(8,128)(2,1)}), bf16[4,8,16,1024]{3,2,1,0:T(8,128)(2,1)S(1)}, u32[]{:S(2)}, u32[]{:S(2)}) %all-to-all-start.7) | async-done | bytes 1048608 | tf_op jit(solution)/shard_map/all_to_all | solution.py:35
  262.4 0.1 copy.42
  262.5 1.2 fusion.17
  (35 shorter events, 0.6 us)
Async XLA Ops:
  0.0 2.0 copy-start
  37.8 23.1 %copy-start.2 = (bf16[1,256,1024]{2,1,0:T(8,128)(2,1)S(1)}, bf16[1,256,1024]{2,1,0:T(8,128)(2,1)}, u32[]{:S(2)}) copy-start(bf16[1,256,1024]{2,1,0:T(8,128)(2,1)} %param.6) | copy-start | bytes 1572868
  106.1 25.0 %collective-permute-start = (bf16[8,1,64,1024]{3,2,0,1:T(8,128)(2,1)S(1)}, bf16[8,1,64,1024]{3,2,0,1:T(8,128)(2,1)S(1)}, u32[]{:S(2)}, u32[]{:S(2)}) collective-permute-start(bf16[8,1,64,1024]{3,2,0,1:T(8,128)(2,1)S(1)} %bitcast.118), channel_id=1, source_target_pairs={{0,1},{1,2},{2,3},{3,0},{4,5},{5,6},{6,7},{7,4},{8,9},{9,10},{10,1... | collective-permute-start | bytes 3145736 | tf_op jit(solution)/shard_map/ppermute | solution.py:20
  106.8 37.9 %collective-permute-start.1 = (bf16[8,1,64,1024]{3,2,0,1:T(8,128)(2,1)S(1)}, bf16[8,1,64,1024]{3,2,0,1:T(8,128)(2,1)}, u32[]{:S(2)}, u32[]{:S(2)}) collective-permute-start(bf16[8,1,64,1024]{3,2,0,1:T(8,128)(2,1)S(1)} %bitcast.119), channel_id=1, source_target_pairs={{0,3},{1,0},{2,1},{3,2},{4,7},{5,4},{6,5},{7,6},{8,11},{9,8},{10,9... | collective-permute-start | bytes 3145736 | tf_op jit(solution)/shard_map/ppermute | solution.py:25
  131.1 24.1 %collective-permute-start.2 = (bf16[8,1,64,1024]{3,2,0,1:T(8,128)(2,1)S(1)}, bf16[8,1,64,1024]{3,2,0,1:T(8,128)(2,1)}, u32[]{:S(2)}, u32[]{:S(2)}) collective-permute-start(bf16[8,1,64,1024]{3,2,0,1:T(8,128)(2,1)S(1)} %collective-permute-done), channel_id=1, source_target_pairs={{0,1},{1,2},{2,3},{3,0},{4,5},{5,6},{6,7},{7,4},{8,9},{9,10},{10,1... | collective-permute-start | bytes 3145736 | tf_op jit(solution)/shard_map/ppermute | solution.py:20
  155.2 10.2 %slice-start.2 = ((s8[7340032]{0:T(1024)(128)(4,1)}), s8[4194304]{0:T(1024)(128)(4,1)S(1)}, s32[]{:S(2)}) async-start(s8[7340032]{0:T(1024)(128)(4,1)} %bitcast.135), calls=%async_computation.10 | async-start | bytes 8388608
  156.7 8.7 %slice-start.3 = ((s8[7340032]{0:T(1024)(128)(4,1)}), s8[3145728]{0:T(1024)(128)(4,1)S(1)}, s32[]{:S(2)}) async-start(s8[7340032]{0:T(1024)(128)(4,1)} %bitcast.135), calls=%async_computation.11 | async-start | bytes 6291456
  156.7 13.3 %slice-start = ((s8[7340032]{0:T(1024)(128)(4,1)}), s8[4194304]{0:T(1024)(128)(4,1)S(1)}, s32[]{:S(2)}) async-start(s8[7340032]{0:T(1024)(128)(4,1)} %bitcast.115), calls=%async_computation.8 | async-start | bytes 8388608
  165.5 4.6 %slice-start.1 = ((s8[7340032]{0:T(1024)(128)(4,1)}), s8[3145728]{0:T(1024)(128)(4,1)S(1)}, s32[]{:S(2)}) async-start(s8[7340032]{0:T(1024)(128)(4,1)} %bitcast.115), calls=%async_computation.9 | async-start | bytes 6291456
  231.4 15.9 %copy-start.3 = (f32[131328]{0:T(1024)S(1)}, f32[131328]{0:T(1024)}, u32[]{:S(2)}) copy-start(f32[131328]{0:T(1024)} %reduce_sum.61) | copy-start | bytes 1575940
  231.4 11.3 %all-to-all-start.6 = ((bf16[8,1,16,1024]{3,2,1,0:T(8,128)(2,1)}), bf16[8,1,16,1024]{3,2,1,0:T(8,128)(2,1)S(1)}, u32[]{:S(2)}, u32[]{:S(2)}) async-start(bf16[8,1,16,1024]{3,2,1,0:T(8,128)(2,1)} %bitcast.39), calls=%async_computation.6 | async-start | bytes 524288 | tf_op jit(solution)/shard_map/all_to_all | solution.py:155
  242.8 21.0 %copy-start.1 = (bf16[1024,512]{1,0:T(8,128)(2,1)S(1)}, bf16[1024,512]{1,0:T(8,128)(2,1)}, u32[]{:S(2)}) copy-start(bf16[1024,512]{1,0:T(8,128)(2,1)} %param.8) | copy-start | bytes 3145732
  243.9 18.5 %all-to-all-start.7 = ((bf16[4,8,16,1024]{3,2,1,0:T(8,128)(2,1)}), bf16[4,8,16,1024]{3,2,1,0:T(8,128)(2,1)S(1)}, u32[]{:S(2)}, u32[]{:S(2)}) async-start(bf16[4,8,16,1024]{3,2,1,0:T(8,128)(2,1)} %broadcast_in_dim.16), calls=%async_computation.7 | async-start | bytes 2097152 | tf_op jit(solution)/shard_map/all_to_all | solution.py:35
